TPU v7x, 32 devices: a whole 2x2x4 slice. The times are simulated.
32 devices in a mesh: grp: 2 (over y), kvp: 4 (over x, core), tp: 4 (over z).
Axes of the slice: x: 2, y: 2, z: 4, core: 2. Of those that a mesh axis runs over, the one named last changes fastest.
Arguments:
- normed: bfloat16 [512, 6144], P('grp', 'kvp'), parts along dimension 0, may hold values from -6 to 6
- w_query: bfloat16 [6144, 6144], P('kvp', 'tp'), may hold values from -0.078125 to 0.078125
- w_key: bfloat16 [6144, 1024], P('kvp', 'tp'), may hold values from -0.078125 to 0.078125
- w_value: bfloat16 [6144, 1024], P('kvp', 'tp'), may hold values from -0.078125 to 0.078125
- w_out: bfloat16 [6144, 6144], P('tp', 'kvp'), may hold values from -0.078125 to 0.078125
- key_cache: bfloat16 [8, 1024, 128, 128], P('tp', ('grp', 'kvp')), parts along dimension 1, may hold values from -128 to 128
- value_cache: bfloat16 [8, 1024, 128, 128], P('tp', ('grp', 'kvp')), parts along dimension 1, may hold values from -6 to 6
- lengths: int32 [512], P('grp'), parts along dimension 0, may hold values from 1 to 12288, as said below
- page_table: int32 [512, 96], P('grp'), parts along dimension 0, may hold values from -1 to 511, as said below
Outputs:
- attended: bfloat16 [512, 6144], P(('grp', 'tp'), 'kvp'), parts along dimension 0
There are 2 independent parts, one for each index of `grp`. A program takes and returns all parts, laid end to end along the dimension named above; an argument that names none is the same for every part. Nothing has to cross between parts.
Inputs may be any that keep to these rules, and one draw needn't show every extreme that they name: `lengths`: every request has at least one cached token; the longest request fills all 96 entries of its page table. `page_table`: entry [b, j] is a page index exactly when j < ceil(lengths[b] / 128), else -1; no page is named twice. Index kvp = i holds pages i * 128 to (i + 1) * 128 - 1; the pages in use are spread unevenly over kvp.
All inputs are finite; a program needn't handle non-finite values.
Results may differ from a plain program's by a relative error of at most 0.012.
Values may be sent and summed in bfloat16 or wider, within the bound.
A program may use at most 64 MiB of HBM per device.

v0:
```python
import jax
import jax.numpy as jnp
from jax import lax
from jax.sharding import PartitionSpec as P

ROPE_BASE = 1000000.0
NEG = -1e30
TWO_PI_HIGH = 6.28125
TWO_PI_LOW = 0.0019353071795864768


def rotate(x, pos):
    width = x.shape[-1]
    half = width // 2
    freq = ROPE_BASE ** (-(2.0 * jnp.arange(half, dtype=jnp.float32)) / width)
    coarse = lax.optimization_barrier(freq.astype(jnp.bfloat16)).astype(jnp.float32)
    fine = freq - coarse
    pos_e = pos[..., None]
    exact = pos_e * coarse
    turns = jnp.floor(exact / TWO_PI_HIGH)
    angle = exact - turns * TWO_PI_HIGH - turns * TWO_PI_LOW + pos_e * fine
    cosine = jnp.cos(angle)
    sine = jnp.sin(angle)
    first = x[..., :half]
    second = x[..., half:]
    return jnp.concatenate(
        [first * cosine - second * sine, second * cosine + first * sine], axis=-1
    )


def source_merge(received):
    marks, totals, accs = received
    top = jnp.max(marks, axis=0)
    weight = jnp.exp(marks - top[None])
    return (top, jnp.sum(weight * totals, axis=0), jnp.sum(weight[..., None] * accs, axis=0))


def finish(top, total, acc, q_rows, k_rows, v_rows, scale):
    s_new = jnp.einsum("bhgd,bhd->bhg", q_rows, k_rows, preferred_element_type=jnp.float32) * scale
    peak = jnp.maximum(top, s_new)
    w_old = jnp.exp(top - peak)
    w_new = jnp.exp(s_new - peak)
    total = w_old * total + w_new
    acc = w_old[..., None] * acc + w_new[..., None] * v_rows.astype(jnp.float32)[:, :, None, :]
    out = (acc / total[..., None]).astype(jnp.bfloat16)
    return out.reshape(out.shape[0], -1)


def body(normed, w_query, w_key, w_value, w_out, key_cache, value_cache, lengths, page_table):
    batch = normed.shape[0]
    kv_local = key_cache.shape[0]
    pages = key_cache.shape[1]
    page = key_cache.shape[2]
    head_dim = key_cache.shape[3]
    group = w_query.shape[1] // (kv_local * head_dim)
    blocks_max = page_table.shape[1]
    scale = head_dim ** (-0.5)
    rank = lax.axis_index("kvp")
    spread = lax.axis_size("kvp")
    rows = batch // spread
    start = rank * rows
    part_q = jnp.dot(normed, w_query, preferred_element_type=jnp.float32)
    part_k = jnp.dot(normed, w_key, preferred_element_type=jnp.float32)
    part_v = jnp.dot(normed, w_value, preferred_element_type=jnp.float32)
    position = lengths.astype(jnp.float32)
    q_share, k_share, v_share = (
        lax.psum_scatter(part_q, "kvp", scatter_dimension=0, tiled=True),
        lax.psum_scatter(part_k, "kvp", scatter_dimension=0, tiled=True),
        lax.psum_scatter(part_v, "kvp", scatter_dimension=0, tiled=True),
    )
    pos_share = lax.dynamic_slice_in_dim(position, start, rows, 0)
    q_part = rotate(
        q_share.reshape(rows, kv_local, group, head_dim), pos_share[:, None, None]
    ).astype(jnp.bfloat16)
    k_rows = rotate(k_share.reshape(rows, kv_local, head_dim), pos_share[:, None]).astype(
        jnp.bfloat16
    )
    v_rows = v_share.reshape(rows, kv_local, head_dim).astype(jnp.bfloat16)
    q_rot = lax.all_gather(q_part, "kvp", axis=0, tiled=True)
    slot_ids = rank * pages + jnp.arange(pages, dtype=jnp.int32)
    hits = page_table[:, :, None] == slot_ids[None, None, :]
    present = jnp.any(hits, axis=(0, 1))
    request_ids = jnp.arange(batch, dtype=jnp.int32)
    owner = jnp.sum(jnp.where(hits, request_ids[:, None, None], 0), axis=(0, 1))
    block = jnp.sum(
        jnp.where(hits, jnp.arange(blocks_max, dtype=jnp.int32)[None, :, None], 0), axis=(0, 1)
    )
    q_owned = q_rot[owner]
    token_pos = block[:, None] * page + jnp.arange(page, dtype=jnp.int32)[None, :]
    valid = present[:, None] & (token_pos < lengths[owner][:, None])
    scores = (
        jnp.einsum("phgd,hptd->phgt", q_owned, key_cache, preferred_element_type=jnp.float32)
        * scale
    )
    scores = jnp.where(valid[:, None, None, :], scores, NEG)
    slot_top = jnp.max(scores, axis=-1)
    weights = jnp.where(valid[:, None, None, :], jnp.exp(scores - slot_top[..., None]), 0.0)
    slot_total = jnp.sum(weights, axis=-1)
    slot_acc = jnp.einsum(
        "phgt,hptd->phgd",
        weights.astype(jnp.bfloat16),
        value_cache,
        preferred_element_type=jnp.float32,
    )
    belongs = (owner[None, :] == request_ids[:, None]) & present[None, :]
    mask = belongs[:, :, None, None]
    top = jnp.max(jnp.where(mask, slot_top[None], NEG), axis=1)
    factor = jnp.where(mask, jnp.exp(slot_top[None] - top[:, None]), 0.0)
    total = jnp.sum(factor * slot_total[None], axis=1)
    acc = jnp.einsum("bphg,phgd->bhgd", factor, slot_acc, precision=lax.Precision.HIGHEST)
    top, total, acc = source_merge(
        (
            lax.all_to_all(top[None], "kvp", split_axis=1, concat_axis=0, tiled=True),
            lax.all_to_all(total[None], "kvp", split_axis=1, concat_axis=0, tiled=True),
            lax.all_to_all(acc[None], "kvp", split_axis=1, concat_axis=0, tiled=True),
        )
    )
    q_rows = lax.dynamic_slice_in_dim(q_rot, start, rows, 0)
    head_out = finish(top, total, acc, q_rows, k_rows, v_rows, scale)
    terms = jnp.dot(
        lax.all_gather(head_out, "kvp", axis=0, tiled=True),
        w_out,
        preferred_element_type=jnp.float32,
    )
    return lax.psum_scatter(terms, "tp", scatter_dimension=0, tiled=True).astype(jnp.bfloat16)


def solution(mesh):
    return jax.shard_map(
        body,
        mesh=mesh,
        in_specs=(
            P("grp", "kvp"),
            P("kvp", "tp"),
            P("kvp", "tp"),
            P("kvp", "tp"),
            P("tp", "kvp"),
            P("tp", ("grp", "kvp"), None, None),
            P("tp", ("grp", "kvp"), None, None),
            P("grp"),
            P("grp", None),
        ),
        out_specs=P(("grp", "tp"), "kvp"),
        check_vma=False,
    )
```

profile of v0, /device:TPU:0, one launch (start us, length us, event | category | flops | bytes accessed | tf_op | source)
XLA Modules:
  0.0 187.5 jit_solution(7497890433573598699)
XLA Ops:
  6.5 1.1 copy-done
  7.7 2.2 %fusion.49 = f32[256,256]{1,0:T(8,128)} fusion(bf16[256,1536]{1,0:T(8,128)(2,1)S(1)} %copy-done, bf16[1536,256]{1,0:T(8,128)(2,1)} %param.11), kind=kOutput, calls=%fused_computation.77 | convolution fusion | flops 201326592 | bytes 1835008 | tf_op jit(solution)/shard_map/dot_general | solution.py:63
  9.9 4.9 %fusion.48 = f32[256,1536]{1,0:T(8,128)} fusion(bf16[256,1536]{1,0:T(8,128)(2,1)S(1)} %copy-done, bf16[1536,1536]{1,0:T(8,128)(2,1)} %param.10), kind=kOutput, calls=%fused_computation.76 | convolution fusion | flops 1207959552 | bytes 7077888 | tf_op jit(solution)/shard_map/dot_general | solution.py:62
  14.9 1.0 copy-done.2
  15.9 1.1 fusion.50
  17.2 4.6 %fusion.1 = (s32[128]{0:T(128)S(1)}, s32[128]{0:T(128)S(1)}) fusion(s32[128]{0:T(128)S(1)} %iota_add_fusion, s32[256,96]{1,0:T(8,128)S(1)} %copy.63), kind=kLoop, calls=%fused_computation.6 | loop fusion | flops 15728384 | bytes 99840 | tf_op jit(solution)/shard_map/reduce_sum | solution.py:85
  21.8 4.5 %compare_reduce_fusion = pred[128]{0:T(512)(128)(4,1)S(1)} fusion(s32[128]{0:T(128)S(1)} %iota_add_fusion, s32[256,96]{1,0:T(8,128)S(1)} %copy.63), kind=kLoop, calls=%fused_computation.3 | loop fusion | flops 6291328 | bytes 98944 | tf_op jit(solution)/shard_map/reduce_or | solution.py:82
  26.3 1.3 gather_fusion
  28.1 4.7 %reduce-scatter.7.cloned.1.call-done = f32[64,256]{1,0:T(8,128)} async-done(((f32[256,256]{1,0:T(8,128)}), f32[64,256]{1,0:T(8,128)}) %reduce-scatter.7.cloned.1.call-update) | async-done | bytes 65552 | tf_op jit(solution)/shard_map/reduce_scatter | solution.py:68
  32.8 0.9 reshape.362
  33.7 29.7 %reduce-scatter.5.cloned.1.call-done = f32[64,1536]{1,0:T(8,128)} async-done(((f32[256,1536]{1,0:T(8,128)}), f32[64,1536]{1,0:T(8,128)}) %reduce-scatter.5.cloned.1.call-update) | async-done | bytes 393232 | tf_op jit(solution)/shard_map/reduce_scatter | solution.py:67
  63.4 1.1 reshape.361
  65.2 8.0 %all_gather.6 = bf16[256,2,6,128]{3,1,2,0:T(2,128)(2,1)S(1)} all-gather(bf16[64,2,6,128]{3,1,2,0:T(2,128)(2,1)S(1)} %copy.64), channel_id=1, replica_groups=mesh['grp'=2,'kvp'=4,'tp'=4] {'kvp'}, dimensions={0}, use_global_device_ids=true | all-gather | bytes 983040 | tf_op jit(solution)/shard_map/all_gather | solution.py:79
  73.2 1.4 gather_fusion.1
  74.6 7.0 %fusion.47 = (f32[128,2,6]{2,1,0:T(2,128)S(1)}, f32[128,2,6,128]{3,2,1,0:T(8,128)S(1)}) fusion(bf16[2,128,128,128]{3,2,1,0:T(8,128)(2,1)} %param.14, bf16[128,2,6,128]{3,1,2,0:T(2,128)(2,1)S(1)} %gather_fusion.1, pred[128,128]{1,0:T(8,128)(4,1)S(1)} %fusion.30), kind=kOutput, calls=%fused_computation.75 | convolution fusion | flops 50919936 | bytes 9590784 | tf_op jit(solution)/shard_map/phgd,hptd->phgt/dot_general | solution.py:92
  81.7 0.8 fusion.14
  83.1 0.9 multiply_reduce_fusion
  84.2 1.0 reshape.384
  85.1 3.3 %all-to-all-start.2 = ((f32[4,1,768]{2,1,0:T(1,128)}), f32[4,1,768]{2,1,0:T(1,128)S(1)}, u32[]{:S(2)}, u32[]{:S(2)}) async-start(f32[4,1,768]{2,1,0:T(1,128)} %reshape.384), calls=%async_computation.5 | async-start | bytes 24576 | tf_op jit(solution)/shard_map/all_to_all | solution.py:114
  88.4 6.7 %fusion.2 = f32[128,2,6,128]{3,2,1,0:T(8,128)} fusion(bf16[2,128,128,128]{3,2,1,0:T(8,128)(2,1)} %param.15, f32[128,2,6,128]{3,2,1,0:T(8,128)S(1)} %get-tuple-element.19, f32[128,2,6]{2,1,0:T(2,128)S(1)} %get-tuple-element.18, pred[128,128]{1,0:T(8,128)(4,1)S(1)} %fusion.30), kind=kOutput, calls=%fused_computation.7 | convolution fusion | flops 50921472 | bytes 9984000 | tf_op jit(solution)/shard_map/phgt,hptd->phgd/dot_general | solution.py:99
  95.3 1.0 reshape.382
  96.2 3.4 %all-to-all-start = ((f32[4,1,768]{2,1,0:T(1,128)}), f32[4,1,768]{2,1,0:T(1,128)S(1)}, u32[]{:S(2)}, u32[]{:S(2)}) async-start(f32[4,1,768]{2,1,0:T(1,128)} %reshape.382), calls=%async_computation.1 | async-start | bytes 24576 | tf_op jit(solution)/shard_map/all_to_all | solution.py:113
  99.7 3.4 %fusion.7 = f32[1,256,2,6,128]{1,4,3,2,0:T(8,128)S(1)} fusion(f32[128,2,6,128]{3,2,1,0:T(8,128)} %fusion.2, f32[256,2,6]{0,2,1:T(8,128)S(1)} %select_reduce_fusion, f32[128,2,6]{0,2,1:T(8,128)S(1)} %copy.67, pred[256,128]{1,0:T(8,128)(4,1)S(1)} %fusion.28), kind=kOutput, calls=%fused_computation.16 | convolution fusion | flops 604766208 | bytes 2410496 | tf_op jit(solution)/shard_map/bphg,phgd->bhgd/dot_general | solution.py:110
  103.1 2.2 %copy.74 = f32[1,256,2,6,128]{4,2,3,0,1:T(2,128)} copy(f32[1,256,2,6,128]{1,4,3,2,0:T(8,128)S(1)} %fusion.7) | data formatting | bytes 3145728 | tf_op jit(solution)/shard_map/broadcast_in_dim | solution.py:115
  105.2 3.6 %all-to-all-start.1 = ((f32[1,256,2,6,128]{4,2,3,0,1:T(2,128)}), f32[1,256,2,6,128]{4,2,3,0,1:T(2,128)S(1)}, u32[]{:S(2)}, u32[]{:S(2)}) async-start(f32[1,256,2,6,128]{4,2,3,0,1:T(2,128)} %copy.74), calls=%async_computation.3 | async-start | bytes 3145728 | tf_op jit(solution)/shard_map/all_to_all | solution.py:115
  109.2 0.8 copy_bitcast_fusion
  112.3 0.7 reduce.1
  113.9 14.9 %all-to-all-done.1 = f32[1,256,2,6,128]{4,2,3,0,1:T(2,128)S(1)} async-done(((f32[1,256,2,6,128]{4,2,3,0,1:T(2,128)}), f32[1,256,2,6,128]{4,2,3,0,1:T(2,128)S(1)}, u32[]{:S(2)}, u32[]{:S(2)}) %all-to-all-start.1) | async-done | bytes 1572896 | tf_op jit(solution)/shard_map/all_to_all | solution.py:115
  130.2 7.9 %all_gather.7 = bf16[256,1536]{1,0:T(8,128)(2,1)S(1)} all-gather(bf16[64,1536]{1,0:T(8,128)(2,1)S(1)} %convert_element_type.52), channel_id=1, replica_groups=mesh['grp'=2,'kvp'=4,'tp'=4] {'kvp'}, dimensions={0}, use_global_device_ids=true | all-gather | bytes 983040 | tf_op jit(solution)/shard_map/all_gather | solution.py:121
  138.1 4.9 %fusion.51 = f32[256,1536]{1,0:T(8,128)} fusion(bf16[256,1536]{1,0:T(8,128)(2,1)S(1)} %all_gather.7, bf16[1536,1536]{1,0:T(8,128)(2,1)} %param.13), kind=kOutput, calls=%fused_computation.79 | convolution fusion | flops 1207959552 | bytes 7077888 | tf_op jit(solution)/shard_map/dot_general | solution.py:120
  143.0 36.3 %reduce-scatter.11.cloned.1.call-done = f32[64,1536]{1,0:T(8,128)} async-done(((f32[256,1536]{1,0:T(8,128)}), f32[64,1536]{1,0:T(8,128)}) %reduce-scatter.11.cloned.1.call-update) | async-done | bytes 393232 | tf_op jit(solution)/shard_map/reduce_scatter | solution.py:125
  179.3 1.7 convert_element_type.53
  (61 shorter events, 7.2 us)
Async XLA Ops:
  6.5 1.1 copy-start
  6.5 26.3 %reduce-scatter.7.cloned.1.call-start = ((), (), s32[]{:S(2)}) async-start(), calls=%async_computation.8 | async-start | bytes 327680 | tf_op jit(solution)/shard_map/reduce_scatter | solution.py:68
  9.9 53.6 %reduce-scatter.5.cloned.1.call-start = ((), (), s32[]{:S(2)}) async-start(), calls=%async_computation.7 | async-start | bytes 1966080 | tf_op jit(solution)/shard_map/reduce_scatter | solution.py:67
  14.8 1.1 copy-start.2
  14.8 2.3 %copy-start.3 = (s32[256,96]{0,1:T(8,128)S(1)}, s32[256,96]{0,1:T(8,128)}, u32[]{:S(2)}) copy-start(s32[256,96]{0,1:T(8,128)} %param.17) | copy-start | bytes 294916
  14.8 11.5 %copy-start.1 = (s32[256]{0:T(256)S(1)}, s32[256]{0:T(256)}, u32[]{:S(2)}) copy-start(s32[256]{0:T(256)} %param.16) | copy-start | bytes 3076
  14.9 94.3 %reduce-scatter.9.cloned.1.call-start = ((), (), s32[]{:S(2)}) async-start(), calls=%async_computation.9 | async-start | bytes 327680 | tf_op jit(solution)/shard_map/reduce_scatter | solution.py:69
  85.1 11.1 %all-to-all-start.2 = ((f32[4,1,768]{2,1,0:T(1,128)}), f32[4,1,768]{2,1,0:T(1,128)S(1)}, u32[]{:S(2)}, u32[]{:S(2)}) async-start(f32[4,1,768]{2,1,0:T(1,128)} %reshape.384), calls=%async_computation.5 | async-start | bytes 24576 | tf_op jit(solution)/shard_map/all_to_all | solution.py:114
  96.2 9.0 %all-to-all-start = ((f32[4,1,768]{2,1,0:T(1,128)}), f32[4,1,768]{2,1,0:T(1,128)S(1)}, u32[]{:S(2)}, u32[]{:S(2)}) async-start(f32[4,1,768]{2,1,0:T(1,128)} %reshape.382), calls=%async_computation.1 | async-start | bytes 24576 | tf_op jit(solution)/shard_map/all_to_all | solution.py:113
  105.2 23.6 %all-to-all-start.1 = ((f32[1,256,2,6,128]{4,2,3,0,1:T(2,128)}), f32[1,256,2,6,128]{4,2,3,0,1:T(2,128)S(1)}, u32[]{:S(2)}, u32[]{:S(2)}) async-start(f32[1,256,2,6,128]{4,2,3,0,1:T(2,128)} %copy.74), calls=%async_computation.3 | async-start | bytes 3145728 | tf_op jit(solution)/shard_map/all_to_all | solution.py:115
  108.8 70.5 %reduce-scatter.11.cloned.1.call-start = ((), (), s32[]{:S(2)}) async-start(), calls=%async_computation.10 | async-start | bytes 1966080 | tf_op jit(solution)/shard_map/reduce_scatter | solution.py:125
Sparse Core Ops, SparseCore 0:
  10.0 22.7 reduce-scatter.6
  35.4 28.0 reduce-scatter.4
  65.9 20.0 reduce-scatter.8
  143.1 36.0 reduce-scatter.10
where the time goes:
time: 188 us; the launch traced here: 187 us
  waiting for transfers between devices  85.7 us (46%)
  matrix products  30.4 us (16%)
  other arithmetic  17.4 us (9%)
  blocking collectives  15.9 us (8%)
  local copies, waits for them, and re-layouts  14.2 us (8%)
  between operations  13.5 us (7%)
  starting transfers between devices  10.4 us (6%)
    reduce_scatter x1, waiting for transfers between devices, body(): lax.psum_scatter(terms, 'tp', scatter_dimension=0, tiled=True)  36.3 us
    reduce_scatter x1, waiting for transfers between devices, body(): lax.psum_scatter(part_q, 'kvp', scatter_dimension=0, tiled=True)  29.7 us
    all_to_all x1, waiting for transfers between devices, body(): lax.all_to_all(acc[None], 'kvp', split_axis=1, concat_axis=0, tiled=True)  14.9 us
    all_gather x1, blocking collectives, body(): q_rot = lax.all_gather(q_part, 'kvp', axis=0, tiled=True)  8.04 us
    all_gather x1, blocking collectives, body(): lax.all_gather(head_out, 'kvp', axis=0, tiled=True)  7.9 us
    dot_general x1, matrix products, body(): jnp.einsum('phgd,hptd->phgt', q_owned, key_cache, preferred_element_type=...  6.99 us
    dot_general x1, matrix products, body(): jnp.einsum('phgt,hptd->phgd', weights.astype(jnp.bfloat16), value_cache,...  6.71 us
    unnamed x14, local copies, waits for them, and re-layouts  5.09 us
  transfers between devices with their start and end apart: 7, of which 4 were waited for; matrix products, arithmetic and copies ran while one was open for 26% of the time, Pallas kernels for 0%

commit v1 on v0

--- a/solution.py
+++ b/solution.py
@@ -112,7 +112,12 @@
         (
             lax.all_to_all(top[None], "kvp", split_axis=1, concat_axis=0, tiled=True),
             lax.all_to_all(total[None], "kvp", split_axis=1, concat_axis=0, tiled=True),
-            lax.all_to_all(acc[None], "kvp", split_axis=1, concat_axis=0, tiled=True),
+            jnp.concatenate(
+                lax.all_to_all(
+                    jnp.stack(jnp.split(acc[None], lax.axis_size("kvp"), axis=1)), "kvp", 0, 0
+                ),
+                axis=0,
+            ),
         )
     )
     q_rows = lax.dynamic_slice_in_dim(q_rot, start, rows, 0)

time: 188 us -> 171 us (0.910)
  waiting for transfers between devices: 85.7 us -> 66.8 us
  matrix products: 30.4 us -> 26.1 us
  local copies, waits for them, and re-layouts: 14.2 us -> 17.5 us
  other arithmetic: 17.4 us -> 20.3 us
    reduce_scatter x1, waiting for transfers between devices: 29.7 us -> 17.5 us  [body(): lax.psum_scatter(part_q, 'kvp', scatter_dimension=0, tiled=True)]
    reduce_scatter x1, waiting for transfers between devices: 4.74 us -> 0.02 us  [body(): lax.psum_scatter(part_k, 'kvp', scatter_dimension=0, tiled=True)]
    another operation x0 -> x2, local copies, waits for them, and re-layouts: none -> 4.66 us  [body(): jnp.stack(jnp.split(acc[None], lax.axis_size('kvp'), axis=1))]
    another operation x2 -> x3, other arithmetic: 0.4 us -> 3.45 us  [the longest x1 3.05 us: body(): jnp.stack(jnp.split(acc[None], lax.axis_size('kvp'), axis=1))]
    broadcast_in_dim x1 -> x0, local copies, waits for them, and re-layouts: 2.17 us -> none  [body(): acc[None]]
    dot_general x1, matrix products: 6.71 us -> 4.73 us  [body(): jnp.einsum('phgt,hptd->phgd', weights.astype(jnp.bfloat16), value_cache,...]
    all_to_all x1, waiting for transfers between devices: 14.9 us -> 12.9 us  [body(): lax.all_to_all(jnp.stack(jnp.split(acc[None], lax.axis_size('kvp'), axis=...]
    unnamed x14 -> x19, local copies, waits for them, and re-layouts: 5.09 us -> 5.21 us
  transfers between devices with their start and end apart: 7 -> 7, of which waited for: 4 -> 3; matrix products, arithmetic and copies ran while one was open for 26% -> 29% of each run, Pallas kernels for 0% -> 0%
where the time goes in v1:
time: 171 us; the launch traced here: 170 us
  waiting for transfers between devices  66.8 us (39%)
  matrix products  26.1 us (15%)
  other arithmetic  20.3 us (12%)
  local copies, waits for them, and re-layouts  17.5 us (10%)
  blocking collectives  15.9 us (9%)
  between operations  13.5 us (8%)
  starting transfers between devices  10.4 us (6%)
    reduce_scatter x1, waiting for transfers between devices, body(): lax.psum_scatter(terms, 'tp', scatter_dimension=0, tiled=True)  36.3 us
    reduce_scatter x1, waiting for transfers between devices, body(): lax.psum_scatter(part_q, 'kvp', scatter_dimension=0, tiled=True)  17.5 us
    all_to_all x1, waiting for transfers between devices, body(): lax.all_to_all(jnp.stack(jnp.split(acc[None], lax.axis_size('kvp'), axis=...  12.9 us
    all_gather x1, blocking collectives, body(): q_rot = lax.all_gather(q_part, 'kvp', axis=0, tiled=True)  8.04 us
    all_gather x1, blocking collectives, body(): lax.all_gather(head_out, 'kvp', axis=0, tiled=True)  7.9 us
    dot_general x1, matrix products, body(): jnp.einsum('phgd,hptd->phgt', q_owned, key_cache, preferred_element_type=...  6.99 us
    unnamed x19, local copies, waits for them, and re-layouts  5.21 us
    dot_general x1, matrix products, body(): jnp.dot(lax.all_gather(head_out, 'kvp', axis=0, tiled=True), w_out, prefe...  4.89 us
  transfers between devices with their start and end apart: 7, of which 3 were waited for; matrix products, arithmetic and copies ran while one was open for 29% of the time, Pallas kernels for 0%

profile of v1, /device:TPU:0, one launch (start us, length us, event | category | flops | bytes accessed | tf_op | source)
XLA Modules:
  0.0 170.4 jit_solution(18085106761838069363)
XLA Ops:
  6.5 1.1 copy-done
  7.7 4.9 %fusion.49 = f32[256,1536]{1,0:T(8,128)} fusion(bf16[256,1536]{1,0:T(8,128)(2,1)S(1)} %copy-done, bf16[1536,1536]{1,0:T(8,128)(2,1)} %param.10), kind=kOutput, calls=%fused_computation.81 | convolution fusion | flops 1207959552 | bytes 7077888 | tf_op jit(solution)/shard_map/dot_general | solution.py:62
  12.6 1.1 fusion.51
  13.8 1.1 fusion.50
  15.1 4.6 %fusion.1 = (s32[128]{0:T(128)S(1)}, s32[128]{0:T(128)S(1)}) fusion(s32[128]{0:T(128)S(1)} %iota_add_fusion, s32[256,96]{1,0:T(8,128)S(1)} %copy.62), kind=kLoop, calls=%fused_computation.6 | loop fusion | flops 15728384 | bytes 99840 | tf_op jit(solution)/shard_map/reduce_sum | solution.py:85
  19.6 4.5 %compare_reduce_fusion = pred[128]{0:T(512)(128)(4,1)S(1)} fusion(s32[128]{0:T(128)S(1)} %iota_add_fusion, s32[256,96]{1,0:T(8,128)S(1)} %copy.62), kind=kLoop, calls=%fused_computation.3 | loop fusion | flops 6291328 | bytes 98944 | tf_op jit(solution)/shard_map/reduce_or | solution.py:82
  24.2 1.3 gather_fusion
  26.0 17.5 %reduce-scatter.5.cloned.1.call-done = f32[64,1536]{1,0:T(8,128)} async-done(((f32[256,1536]{1,0:T(8,128)}), f32[64,1536]{1,0:T(8,128)}) %reduce-scatter.5.cloned.1.call-update) | async-done | bytes 393232 | tf_op jit(solution)/shard_map/reduce_scatter | solution.py:67
  43.4 1.1 reshape.358
  45.1 8.0 %all_gather.6 = bf16[256,2,6,128]{3,1,2,0:T(2,128)(2,1)S(1)} all-gather(bf16[64,2,6,128]{3,1,2,0:T(2,128)(2,1)S(1)} %copy.63), channel_id=1, replica_groups=mesh['grp'=2,'kvp'=4,'tp'=4] {'kvp'}, dimensions={0}, use_global_device_ids=true | all-gather | bytes 983040 | tf_op jit(solution)/shard_map/all_gather | solution.py:79
  53.2 0.9 copy-done.2
  54.1 1.4 gather_fusion.1
  55.5 7.0 %fusion.48 = (f32[128,2,6]{2,1,0:T(2,128)S(1)}, f32[128,2,6,128]{3,2,1,0:T(8,128)S(1)}) fusion(bf16[2,128,128,128]{3,2,1,0:T(8,128)(2,1)} %param.14, bf16[128,2,6,128]{3,1,2,0:T(2,128)(2,1)S(1)} %gather_fusion.1, pred[128,128]{1,0:T(8,128)(4,1)S(1)} %fusion.31), kind=kOutput, calls=%fused_computation.80 | convolution fusion | flops 50919936 | bytes 9590784 | tf_op jit(solution)/shard_map/phgd,hptd->phgt/dot_general | solution.py:92
  63.9 0.9 multiply_reduce_fusion
  65.1 1.0 reshape.382
  66.0 3.4 %all-to-all-start.2 = ((f32[4,1,768]{2,1,0:T(1,128)}), f32[4,1,768]{2,1,0:T(1,128)S(1)}, u32[]{:S(2)}, u32[]{:S(2)}) async-start(f32[4,1,768]{2,1,0:T(1,128)} %reshape.382), calls=%async_computation.5 | async-start | bytes 24576 | tf_op jit(solution)/shard_map/all_to_all | solution.py:114
  69.5 4.7 %fusion.2 = f32[128,2,6,128]{3,2,1,0:T(8,128)S(1)} fusion(bf16[2,128,128,128]{3,2,1,0:T(8,128)(2,1)} %param.15, f32[128,2,6,128]{3,2,1,0:T(8,128)S(1)} %get-tuple-element.23, f32[128,2,6]{2,1,0:T(2,128)S(1)} %get-tuple-element.22, pred[128,128]{1,0:T(8,128)(4,1)S(1)} %fusion.31), kind=kOutput, calls=%fused_computation.7 | convolution fusion | flops 50921472 | bytes 9984000 | tf_op jit(solution)/shard_map/phgt,hptd->phgd/dot_general | solution.py:99
  74.2 2.2 %fusion.8 = f32[1,256,2,6,128]{1,4,3,2,0:T(8,128)S(1)} fusion(f32[128,2,6,128]{3,2,1,0:T(8,128)S(1)} %fusion.2, f32[256,2,6]{0,2,1:T(8,128)S(1)} %select_reduce_fusion, f32[128,2,6]{0,2,1:T(8,128)S(1)} %copy.66, pred[256,128]{1,0:T(8,128)(4,1)S(1)} %fusion.29), kind=kOutput, calls=%fused_computation.18 | convolution fusion | flops 604766208 | bytes 2410496 | tf_op jit(solution)/shard_map/bphg,phgd->bhgd/dot_general | solution.py:110
  76.4 1.4 slice_bitcast_fusion.3
  78.0 1.0 reshape.380
  78.9 3.2 %all-to-all-start = ((f32[4,1,768]{2,1,0:T(1,128)}), f32[4,1,768]{2,1,0:T(1,128)S(1)}, u32[]{:S(2)}, u32[]{:S(2)}) async-start(f32[4,1,768]{2,1,0:T(1,128)} %reshape.380), calls=%async_computation.1 | async-start | bytes 24576 | tf_op jit(solution)/shard_map/all_to_all | solution.py:113
  82.2 3.0 %pad_maximum_fusion = f32[4,1,64,2,6,128]{2,5,4,3,1,0:T(8,128)} fusion(f32[1,1,64,2,6,128]{2,5,4,3,1,0:T(8,128)S(1)} %get-tuple-element.13, f32[1,1,64,2,6,128]{2,5,4,3,1,0:T(8,128)S(1)} %get-tuple-element.14, f32[1,1,64,2,6,128]{2,5,4,3,1,0:T(8,128)} %get-tuple-element.15, f32[1,1,64,2,6,128]{2,5,4,3,1,0:T(8,128)S(1)} %get-tuple-element.12), kind=kLoop, calls=%fused_computation.11 | loop fusion | flops 1179648 | bytes 3145728 | tf_op jit(solution)/shard_map/stack | solution.py:117
  85.3 3.2 %copy.73 = f32[4,1,64,2,6,128]{5,2,4,3,1,0:T(8,128)} copy(f32[4,1,64,2,6,128]{2,5,4,3,1,0:T(8,128)} %pad_maximum_fusion) | data formatting | bytes 3145728 | tf_op jit(solution)/shard_map/stack | solution.py:117
  88.5 3.6 %all-to-all-start.1 = ((f32[4,1,64,2,6,128]{5,2,4,3,1,0:T(8,128)}), f32[4,1,64,2,6,128]{5,2,4,3,1,0:T(8,128)S(1)}, u32[]{:S(2)}, u32[]{:S(2)}) async-start(f32[4,1,64,2,6,128]{5,2,4,3,1,0:T(8,128)} %copy.73), calls=%async_computation.3 | async-start | bytes 3145728 | tf_op jit(solution)/shard_map/all_to_all | solution.py:116
  92.1 0.8 convert_convert_fusion
  93.1 0.9 reshape.359
  94.3 1.1 constant_dynamic-slice_fusion
  99.1 12.9 %all-to-all-done.1 = f32[4,1,64,2,6,128]{5,2,4,3,1,0:T(8,128)S(1)} async-done(((f32[4,1,64,2,6,128]{5,2,4,3,1,0:T(8,128)}), f32[4,1,64,2,6,128]{5,2,4,3,1,0:T(8,128)S(1)}, u32[]{:S(2)}, u32[]{:S(2)}) %all-to-all-start.1) | async-done | bytes 1572896 | tf_op jit(solution)/shard_map/all_to_all | solution.py:116
  113.1 7.9 %all_gather.7 = bf16[256,1536]{1,0:T(8,128)(2,1)S(1)} all-gather(bf16[64,1536]{1,0:T(8,128)(2,1)S(1)} %copy.88), channel_id=1, replica_groups=mesh['grp'=2,'kvp'=4,'tp'=4] {'kvp'}, dimensions={0}, use_global_device_ids=true | all-gather | bytes 983040 | tf_op jit(solution)/shard_map/all_gather | solution.py:126
  121.0 4.9 %fusion.52 = f32[256,1536]{1,0:T(8,128)} fusion(bf16[256,1536]{1,0:T(8,128)(2,1)S(1)} %all_gather.7, bf16[1536,1536]{1,0:T(8,128)(2,1)} %param.13), kind=kOutput, calls=%fused_computation.84 | convolution fusion | flops 1207959552 | bytes 7077888 | tf_op jit(solution)/shard_map/dot_general | solution.py:125
  125.9 36.3 %reduce-scatter.11.cloned.1.call-done = f32[64,1536]{1,0:T(8,128)} async-done(((f32[256,1536]{1,0:T(8,128)}), f32[64,1536]{1,0:T(8,128)}) %reduce-scatter.11.cloned.1.call-update) | async-done | bytes 393232 | tf_op jit(solution)/shard_map/reduce_scatter | solution.py:130
  162.2 1.7 convert_element_type.53
  (68 shorter events, 8.3 us)
Async XLA Ops:
  6.5 1.1 copy-start
  6.5 6.1 %copy-start.3 = (bf16[1536,256]{1,0:T(8,128)(2,1)S(1)}, bf16[1536,256]{1,0:T(8,128)(2,1)}, u32[]{:S(2)}) copy-start(bf16[1536,256]{1,0:T(8,128)(2,1)} %param.12) | copy-start | bytes 2359300
  6.5 36.9 %reduce-scatter.5.cloned.1.call-start = ((), (), s32[]{:S(2)}) async-start(), calls=%async_computation.7 | async-start | bytes 1966080 | tf_op jit(solution)/shard_map/reduce_scatter | solution.py:67
  12.5 1.2 copy-start.4
  12.5 2.4 %copy-start.5 = (s32[256,96]{0,1:T(8,128)S(1)}, s32[256,96]{0,1:T(8,128)}, u32[]{:S(2)}) copy-start(s32[256,96]{0,1:T(8,128)} %param.17) | copy-start | bytes 294916
  12.5 11.6 %copy-start.1 = (s32[256]{0:T(256)S(1)}, s32[256]{0:T(256)}, u32[]{:S(2)}) copy-start(s32[256]{0:T(256)} %param.16) | copy-start | bytes 3076
  12.6 79.5 %reduce-scatter.9.cloned.1.call-start = ((), (), s32[]{:S(2)}) async-start(), calls=%async_computation.9 | async-start | bytes 327680 | tf_op jit(solution)/shard_map/reduce_scatter | solution.py:69
  13.7 79.3 %reduce-scatter.7.cloned.1.call-start = ((), (), s32[]{:S(2)}) async-start(), calls=%async_computation.8 | async-start | bytes 327680 | tf_op jit(solution)/shard_map/reduce_scatter | solution.py:68
  53.2 0.9 copy-start.2
  66.0 12.9 %all-to-all-start.2 = ((f32[4,1,768]{2,1,0:T(1,128)}), f32[4,1,768]{2,1,0:T(1,128)S(1)}, u32[]{:S(2)}, u32[]{:S(2)}) async-start(f32[4,1,768]{2,1,0:T(1,128)} %reshape.382), calls=%async_computation.5 | async-start | bytes 24576 | tf_op jit(solution)/shard_map/all_to_all | solution.py:114
  78.9 9.5 %all-to-all-start = ((f32[4,1,768]{2,1,0:T(1,128)}), f32[4,1,768]{2,1,0:T(1,128)S(1)}, u32[]{:S(2)}, u32[]{:S(2)}) async-start(f32[4,1,768]{2,1,0:T(1,128)} %reshape.380), calls=%async_computation.1 | async-start | bytes 24576 | tf_op jit(solution)/shard_map/all_to_all | solution.py:113
  88.5 23.6 %all-to-all-start.1 = ((f32[4,1,64,2,6,128]{5,2,4,3,1,0:T(8,128)}), f32[4,1,64,2,6,128]{5,2,4,3,1,0:T(8,128)S(1)}, u32[]{:S(2)}, u32[]{:S(2)}) async-start(f32[4,1,64,2,6,128]{5,2,4,3,1,0:T(8,128)} %copy.73), calls=%async_computation.3 | async-start | bytes 3145728 | tf_op jit(solution)/shard_map/all_to_all | solution.py:116
  92.0 70.2 %reduce-scatter.11.cloned.1.call-start = ((), (), s32[]{:S(2)}) async-start(), calls=%async_computation.10 | async-start | bytes 1966080 | tf_op jit(solution)/shard_map/reduce_scatter | solution.py:130
Sparse Core Ops, SparseCore 0:
  12.7 30.6 reduce-scatter.4
  45.9 20.0 reduce-scatter.8
  68.5 20.0 reduce-scatter.6
  126.1 36.0 reduce-scatter.10
